TPU v7x, 256 devices: a 8x8x2 block of a 8x8x16 slice. The times are simulated.
256 devices in a mesh: groups: 2 (over z), dap: 128 (over x, y, core).
Axes of the slice: x: 8, y: 8, z: 2, core: 2. Of those that a mesh axis runs over, the one named last changes fastest.
The devices are a block of a 8x8x16 slice.
Arguments:
- homolog_tensor: bfloat16 [1024, 256, 256], P(('groups', 'dap')), parts along dimension 0, may hold values from -1 to 1
- couple_tensor: bfloat16 [512, 256, 128], P(('groups', 'dap')), parts along dimension 0, may hold values from -6 to 6
- horizontal_drop_filter: int32 [512, 256], P('groups'), parts along dimension 0, may hold values 0 or 1
- couple_offset_matrix: bfloat16 [128, 8], replicated, may hold values from -0.29882812 to 0.29882812
- horizontal_attend_matrix: bfloat16 [256, 1024], replicated, may hold values from -0.375 to 0.375
- horizontal_exit_matrix: bfloat16 [256, 256], replicated, may hold values from -0.375 to 0.375
- vertical_attend_matrix: bfloat16 [256, 1024], replicated, may hold values from -0.375 to 0.375
- vertical_exit_matrix: bfloat16 [256, 256], replicated, may hold values from -0.375 to 0.375
- averaged_product_flanks: bfloat16 [256, 64], replicated, may hold values from -0.375 to 0.375
- averaged_product_exit: bfloat16 [1024, 128], replicated, may hold values from -1 to 1
Outputs:
- alignment_output: bfloat16 [1024, 256, 256], P('groups', 'dap'), parts along dimension 0
- pair_output_state: bfloat16 [512, 256, 128], P(('groups', 'dap')), parts along dimension 0
There are 2 independent parts, one for each index of `groups`. A program takes and returns all parts, laid end to end along the dimension named above; an argument that names none is the same for every part. Nothing has to cross between parts.
All inputs are finite; a program needn't handle non-finite values.
Results may differ from a plain program's by a relative error of at most 0.012.
Values may be sent and summed in bfloat16 or wider, within the bound.
A program may use at most 64 MiB of HBM per device.

v0:
```python
import jax
import jax.numpy as jnp
from jax import lax
from jax.sharding import Mesh
from jax.sharding import PartitionSpec as P

HEAD_NUMBER = 8
HEAD_WIDTH = 32
FACTOR_FEATURES = 32
DAP = ("dap_0", "dap_1", "dap_2")
GROUPS_DAP = ("groups", "dap_0", "dap_1", "dap_2")


def joined_along(tiles, dim):
    tiles = jnp.moveaxis(tiles, 0, dim)
    dims = tiles.shape
    return tiles.reshape(*dims[:dim], dims[dim] * dims[dim + 1], *dims[dim + 2 :])


def stacked_from(shard, axes, order):
    tiles = shard[None]
    for k in order:
        tiles = lax.all_gather(tiles, axes[k], axis=0, tiled=True)
    carried = [lax.axis_size(axes[k]) for k in reversed(order)]
    tiles = tiles.reshape(*carried, *shard.shape)
    turned = sorted(range(len(order)), key=lambda place: order[len(order) - 1 - place])
    return tiles.transpose(*turned, *range(len(order), tiles.ndim)).reshape(-1, *shard.shape)


def gather_axes(shard, axes, order, dim):
    return joined_along(stacked_from(shard, axes, order), dim)


def standardise_features(values):
    values = values.astype(jnp.float32)
    center = values - jnp.mean(values, axis=-1, keepdims=True)
    spread = jnp.mean(center * center, axis=-1, keepdims=True)
    return center * lax.rsqrt(spread + 1e-05)


def attend(normed, w_qkvg, w_out, bias):
    batch, length = (normed.shape[0], normed.shape[1])
    proj = jnp.einsum("blc,cf->blf", normed, w_qkvg, preferred_element_type=jnp.float32)
    proj = proj.reshape(batch, length, 4, HEAD_NUMBER, HEAD_WIDTH)
    query = (proj[:, :, 0] * HEAD_WIDTH ** (-0.5)).astype(jnp.bfloat16)
    keys = proj[:, :, 1].astype(jnp.bfloat16)
    values = proj[:, :, 2].astype(jnp.bfloat16)
    gate = proj[:, :, 3]
    if bias is None:
        bias = jnp.zeros((HEAD_NUMBER, length, length), jnp.bfloat16)

    def one_head(items):
        qh, kh, vh, bh = items
        scores = jnp.einsum("bid,bjd->bij", qh, kh, preferred_element_type=jnp.float32)
        scores = scores + bh.astype(jnp.float32)[None]
        weights = jax.nn.softmax(scores, axis=-1).astype(jnp.bfloat16)
        return jnp.einsum("bij,bjd->bid", weights, vh, preferred_element_type=jnp.float32)

    heads = lax.map(
        one_head,
        (jnp.moveaxis(query, 2, 0), jnp.moveaxis(keys, 2, 0), jnp.moveaxis(values, 2, 0), bias),
    )
    heads = jnp.moveaxis(heads, 0, 2)
    gated = (
        (jax.nn.sigmoid(gate) * heads)
        .astype(jnp.bfloat16)
        .reshape(batch, length, HEAD_NUMBER * HEAD_WIDTH)
    )
    return jnp.einsum("blk,kc->blc", gated, w_out, preferred_element_type=jnp.float32)


def shards(
    homolog_tensor,
    couple_tensor,
    horizontal_drop_filter,
    couple_offset_matrix,
    horizontal_attend_matrix,
    horizontal_exit_matrix,
    vertical_attend_matrix,
    vertical_exit_matrix,
    averaged_product_flanks,
    averaged_product_exit,
):
    normed_pair = standardise_features(couple_tensor).astype(jnp.bfloat16)
    own_bias = jnp.einsum(
        "ijz,zh->hij", normed_pair, couple_offset_matrix, preferred_element_type=jnp.float32
    ).astype(jnp.bfloat16)
    bias = gather_axes(own_bias, DAP, (0, 1, 2), 1)
    starting_answer = standardise_features(homolog_tensor).astype(jnp.bfloat16)
    perform_refresh = attend(
        starting_answer, horizontal_attend_matrix, horizontal_exit_matrix, bias
    )
    homolog_later = (
        homolog_tensor.astype(jnp.float32)
        + horizontal_drop_filter.astype(jnp.float32) * (1.0 / 0.9) * perform_refresh
    ).astype(jnp.bfloat16)
    incoming_blocks = lax.all_to_all(homolog_later, DAP, split_axis=1, concat_axis=0, tiled=True)
    column_layout = jnp.swapaxes(incoming_blocks, 0, 1)
    perform_refresh = attend(
        standardise_features(column_layout).astype(jnp.bfloat16),
        vertical_attend_matrix,
        vertical_exit_matrix,
        None,
    )
    alignment_output = jnp.swapaxes(
        (column_layout.astype(jnp.float32) + perform_refresh).astype(jnp.bfloat16), 0, 1
    )
    final_result = standardise_features(alignment_output).astype(jnp.bfloat16)
    factors = jnp.einsum(
        "sic,cf->sif", final_result, averaged_product_flanks, preferred_element_type=jnp.float32
    )
    left = factors[..., :FACTOR_FEATURES].astype(jnp.bfloat16)
    right = factors[..., FACTOR_FEATURES:].astype(jnp.bfloat16)
    total = left.shape[0]
    own_rows = left.shape[1]
    piece = lax.all_gather(right, DAP, axis=1, tiled=True)
    outer = jnp.einsum("sic,sjd->ijcd", left, piece, preferred_element_type=jnp.float32) / total
    outer = outer.astype(jnp.bfloat16).reshape(
        own_rows, piece.shape[1], FACTOR_FEATURES * FACTOR_FEATURES
    )
    change = jnp.einsum(
        "ijk,kz->ijz", outer, averaged_product_exit, preferred_element_type=jnp.float32
    )
    pair_output_state = (couple_tensor.astype(jnp.float32) + change).astype(jnp.bfloat16)
    return (alignment_output, pair_output_state)


def solution(mesh):
    torus = Mesh(
        mesh.devices.reshape(mesh.shape["groups"], 8, 8, 2), ("groups", "dap_0", "dap_1", "dap_2")
    )
    return jax.shard_map(
        shards,
        mesh=torus,
        in_specs=(
            P(GROUPS_DAP, None, None),
            P(GROUPS_DAP, None, None),
            P("groups", None),
            P(),
            P(),
            P(),
            P(),
            P(),
            P(),
            P(),
        ),
        out_specs=(P("groups", DAP, None), P(GROUPS_DAP, None, None)),
        check_vma=False,
    )
```

profile of v0, /device:TPU:513, one launch (start us, length us, event | category | flops | bytes accessed | tf_op | source)
XLA Modules:
  0.0 365.0 jit_solution(12928804633516290471)
XLA Ops:
  10.7 20.9 %all-gather = bf16[64,2,256]{2,0,1:T(8,128)(2,1)S(1)} all-gather(bf16[8,2,256]{2,0,1:T(8,128)(2,1)S(1)} %fusion.37), channel_id=2, replica_groups=mesh['groups'=2,'dap_0'=8,'dap_1'=8,'dap_2'=2] {'dap_0'}, dimensions={0}, use_global_device_ids=true | all-gather | bytes 73728 | tf_op jit(solution)/shard_map/all_gather | solution.py:23
  31.7 30.9 %all_gather.13 = bf16[64,8,2,256]{3,1,0,2:T(8,128)(2,1)} all-gather(bf16[8,8,2,256]{3,1,0,2:T(8,128)(2,1)S(1)} %bitcast.194), channel_id=1, replica_groups=mesh['groups'=2,'dap_0'=8,'dap_1'=8,'dap_2'=2] {'dap_1'}, dimensions={0}, use_global_device_ids=true | all-gather | bytes 589824 | tf_op jit(solution)/shard_map/all_gather | solution.py:23
  65.3 2.0 fusion.59
  71.5 27.3 %all-gather.4.cloned.1.call-done = bf16[128,8,2,256]{3,1,0,2:T(8,128)(2,1)} async-done(((bf16[64,8,2,256]{3,1,0,2:T(8,128)(2,1)}), bf16[128,8,2,256]{3,1,0,2:T(8,128)(2,1)}) %all-gather.4.cloned.1.call-update) | async-done | bytes 1048592 | tf_op jit(solution)/shard_map/all_gather | solution.py:23
  101.0 36.0 %while.20 = (s32[]{:T(128)}, f32[8,4,256,32]{2,3,0,1:T(8,128)}, bf16[8,4,256,32]{2,3,0,1:T(8,128)(2,1)}, bf16[8,4,256,32]{2,3,0,1:T(8,128)(2,1)}, bf16[8,256,256...) while((s32[]{:T(128)}, f32[8,4,256,32]{2,3,0,1:T(8,128)}, ...), condition=%wide.region_7.8_spmd, body=%wide.region_4.7_spmd.sunk | while | flops 52233728 | bytes 4533337 | solution.py:59
  103.7 1.9 fusion.105
  108.2 1.9 fusion.105
  112.6 1.9 fusion.105
  117.1 1.8 fusion.105
  121.6 1.8 fusion.105
  126.1 1.8 fusion.105
  130.6 1.8 fusion.105
  135.1 1.9 fusion.105
  136.9 1.8 fusion.54
  141.3 14.5 %all-to-all-start = ((bf16[4,256,256]{2,0,1:T(4,128)(2,1)}), bf16[4,256,256]{2,0,1:T(4,128)(2,1)S(1)}, u32[]{:S(2)}, u32[]{:S(2)}) async-start(bf16[4,256,256]{2,0,1:T(4,128)(2,1)} %copy.59), calls=%async_computation | async-start | bytes 1048576 | tf_op jit(solution)/shard_map/all_to_all | solution.py:97
  156.1 18.9 %all-to-all-done = bf16[4,256,256]{2,0,1:T(4,128)(2,1)S(1)} async-done(((bf16[4,256,256]{2,0,1:T(4,128)(2,1)}), bf16[4,256,256]{2,0,1:T(4,128)(2,1)S(1)}, u32[]{:S(2)}, u32[]{:S(2)}) %all-to-all-start) | async-done | bytes 524320 | tf_op jit(solution)/shard_map/all_to_all | solution.py:97
  177.6 1.8 multiply_convert_fusion.1
  180.3 1.8 copy-done.1
  184.5 2.1 slice_bitcast_fusion
  186.6 73.0 %while.21 = (s32[]{:T(128)}, f32[8,2,512,32]{2,3,0,1:T(8,128)}, bf16[8,2,512,32]{2,3,0,1:T(8,128)(2,1)S(1)}, bf16[8,2,512,32]{2,3,0,1:T(8,128)(2,1)}, bf16[8,2,512,32]{2,3,0,1:T(8,128)(2,1)S(1)}, /*index=5*/s32[]{:T(128)}) while((s32[]{:T(128)}, f32[8,2,512,32]{2,3,0,1:T(8,128)}, bf16[8,2,512,32]{2,3,0,1:T(8,128)(2,1)S(1)}, ...), condition=%wide.region_13.14_spmd, body=%wide.region_10.13_spmd.sunk | while | flops 67108864 | bytes 1507417 | solution.py:59
  190.1 3.8 %dot_general.47 = f32[2,512,32]{2,1,0:T(8,128)} custom-call(bf16[2,512,32]{2,1,0:T(8,128)(2,1)} %bitcast.177, bf16[2,512,32]{2,1,0:T(8,128)(2,1)} %bitcast.176, bf16[2,512,32]{2,1,0:T(8,128)(2,1)} %bitcast.178), custom_call_target="tpu_custom_call" | custom-call | flops 67108864 | bytes 196608 | tf_op jit(solution)/shard_map/while/body/eval_jaxpr/bij,bjd->bid/dot_general | solution.py:57
  199.2 3.8 %dot_general.47 = f32[2,512,32]{2,1,0:T(8,128)} custom-call(bf16[2,512,32]{2,1,0:T(8,128)(2,1)} %bitcast.177, bf16[2,512,32]{2,1,0:T(8,128)(2,1)} %bitcast.176, bf16[2,512,32]{2,1,0:T(8,128)(2,1)} %bitcast.178), custom_call_target="tpu_custom_call" | custom-call | flops 67108864 | bytes 196608 | tf_op jit(solution)/shard_map/while/body/eval_jaxpr/bij,bjd->bid/dot_general | solution.py:57
  208.3 3.8 %dot_general.47 = f32[2,512,32]{2,1,0:T(8,128)} custom-call(bf16[2,512,32]{2,1,0:T(8,128)(2,1)} %bitcast.177, bf16[2,512,32]{2,1,0:T(8,128)(2,1)} %bitcast.176, bf16[2,512,32]{2,1,0:T(8,128)(2,1)} %bitcast.178), custom_call_target="tpu_custom_call" | custom-call | flops 67108864 | bytes 196608 | tf_op jit(solution)/shard_map/while/body/eval_jaxpr/bij,bjd->bid/dot_general | solution.py:57
  217.4 3.8 %dot_general.47 = f32[2,512,32]{2,1,0:T(8,128)} custom-call(bf16[2,512,32]{2,1,0:T(8,128)(2,1)} %bitcast.177, bf16[2,512,32]{2,1,0:T(8,128)(2,1)} %bitcast.176, bf16[2,512,32]{2,1,0:T(8,128)(2,1)} %bitcast.178), custom_call_target="tpu_custom_call" | custom-call | flops 67108864 | bytes 196608 | tf_op jit(solution)/shard_map/while/body/eval_jaxpr/bij,bjd->bid/dot_general | solution.py:57
  226.6 3.8 %dot_general.47 = f32[2,512,32]{2,1,0:T(8,128)} custom-call(bf16[2,512,32]{2,1,0:T(8,128)(2,1)} %bitcast.177, bf16[2,512,32]{2,1,0:T(8,128)(2,1)} %bitcast.176, bf16[2,512,32]{2,1,0:T(8,128)(2,1)} %bitcast.178), custom_call_target="tpu_custom_call" | custom-call | flops 67108864 | bytes 196608 | tf_op jit(solution)/shard_map/while/body/eval_jaxpr/bij,bjd->bid/dot_general | solution.py:57
  235.7 3.8 %dot_general.47 = f32[2,512,32]{2,1,0:T(8,128)} custom-call(bf16[2,512,32]{2,1,0:T(8,128)(2,1)} %bitcast.177, bf16[2,512,32]{2,1,0:T(8,128)(2,1)} %bitcast.176, bf16[2,512,32]{2,1,0:T(8,128)(2,1)} %bitcast.178), custom_call_target="tpu_custom_call" | custom-call | flops 67108864 | bytes 196608 | tf_op jit(solution)/shard_map/while/body/eval_jaxpr/bij,bjd->bid/dot_general | solution.py:57
  244.8 3.8 %dot_general.47 = f32[2,512,32]{2,1,0:T(8,128)} custom-call(bf16[2,512,32]{2,1,0:T(8,128)(2,1)} %bitcast.177, bf16[2,512,32]{2,1,0:T(8,128)(2,1)} %bitcast.176, bf16[2,512,32]{2,1,0:T(8,128)(2,1)} %bitcast.178), custom_call_target="tpu_custom_call" | custom-call | flops 67108864 | bytes 196608 | tf_op jit(solution)/shard_map/while/body/eval_jaxpr/bij,bjd->bid/dot_general | solution.py:57
  253.9 3.8 %dot_general.47 = f32[2,512,32]{2,1,0:T(8,128)} custom-call(bf16[2,512,32]{2,1,0:T(8,128)(2,1)} %bitcast.177, bf16[2,512,32]{2,1,0:T(8,128)(2,1)} %bitcast.176, bf16[2,512,32]{2,1,0:T(8,128)(2,1)} %bitcast.178), custom_call_target="tpu_custom_call" | custom-call | flops 67108864 | bytes 196608 | tf_op jit(solution)/shard_map/while/body/eval_jaxpr/bij,bjd->bid/dot_general | solution.py:57
  259.7 1.8 fusion.55
  264.1 77.3 %all-gather.6.cloned.1.call-done = bf16[512,256,32]{0,2,1:T(8,128)(2,1)} async-done(((bf16[512,2,32]{0,2,1:T(8,128)(2,1)}), bf16[512,256,32]{0,2,1:T(8,128)(2,1)}) %all-gather.6.cloned.1.call-update) | async-done | bytes 8388624 | tf_op jit(solution)/shard_map/all_gather | solution.py:116
  341.4 9.4 %fusion.26 = bf16[2,256,32,32]{2,3,0,1:T(8,128)(2,1)} fusion(bf16[512,256,32]{0,2,1:T(8,128)(2,1)} %all-gather.6.cloned.1.call-done, bf16[512,2,64]{0,2,1:T(8,128)(2,1)S(1)} %convolution_convert_fusion), kind=kOutput, calls=%fused_computation.30 | convolution fusion | flops 537919488 | bytes 9502720 | tf_op jit(solution)/shard_map/sic,sjd->ijcd/dot_general | solution.py:117
  350.8 6.2 %copy.71 = bf16[2,256,32,32]{1,3,2,0:T(8,128)(2,1)S(1)} copy(bf16[2,256,32,32]{2,3,0,1:T(8,128)(2,1)} %fusion.26) | data formatting | bytes 2097152 | tf_op jit(solution)/shard_map/convert_element_type | solution.py:118
  (141 shorter events, 88.3 us)
Async XLA Ops:
  7.2 58.2 %copy-start = (bf16[256,1024]{1,0:T(8,128)(2,1)S(1)}, bf16[256,1024]{1,0:T(8,128)(2,1)}, u32[]{:S(2)}) copy-start(bf16[256,1024]{1,0:T(8,128)(2,1)} %param.18) | copy-start | bytes 1572868
  7.2 91.6 %all-gather.4.cloned.1.call-start = ((), (), s32[]{:S(2)}) async-start(), calls=%async_computation.1 | async-start | bytes 1572864 | tf_op jit(solution)/shard_map/all_gather | solution.py:23
  67.4 3.0 copy-start.2
  67.4 1.1 copy-start.6
  100.9 37.8 %copy-start.3 = (bf16[4,256,256]{2,1,0:T(8,128)(2,1)S(1)}, bf16[4,256,256]{2,1,0:T(8,128)(2,1)}, u32[]{:S(2)}) copy-start(bf16[4,256,256]{2,1,0:T(8,128)(2,1)} %param.14) | copy-start | bytes 1572868
  101.0 37.8 %copy-start.9 = (bf16[256,256]{1,0:T(8,128)(2,1)S(1)}, bf16[256,256]{1,0:T(8,128)(2,1)}, u32[]{:S(2)}) copy-start(bf16[256,256]{1,0:T(8,128)(2,1)} %param.19) | copy-start | bytes 393220
  141.3 38.1 %copy-start.5 = (bf16[256,1024]{1,0:T(8,128)(2,1)S(1)}, bf16[256,1024]{1,0:T(8,128)(2,1)}, u32[]{:S(2)}) copy-start(bf16[256,1024]{1,0:T(8,128)(2,1)} %param.20) | copy-start | bytes 1572868
  141.3 33.6 %all-to-all-start = ((bf16[4,256,256]{2,0,1:T(4,128)(2,1)}), bf16[4,256,256]{2,0,1:T(4,128)(2,1)S(1)}, u32[]{:S(2)}, u32[]{:S(2)}) async-start(bf16[4,256,256]{2,0,1:T(4,128)(2,1)} %copy.59), calls=%async_computation | async-start | bytes 1048576 | tf_op jit(solution)/shard_map/all_to_all | solution.py:97
  155.8 185.6 %all-gather.6.cloned.1.call-start = ((), (), s32[]{:S(2)}) async-start(), calls=%async_computation.2 | async-start | bytes 8454144 | tf_op jit(solution)/shard_map/all_gather | solution.py:116
  180.1 1.9 copy-start.1
  186.6 74.9 %copy-start.8 = (bf16[256,256]{1,0:T(8,128)(2,1)S(1)}, bf16[256,256]{1,0:T(8,128)(2,1)}, u32[]{:S(2)}) copy-start(bf16[256,256]{1,0:T(8,128)(2,1)} %param.21) | copy-start | bytes 393220
  259.7 2.4 copy-start.10
  350.8 6.2 %copy-start.4 = (bf16[2,256,128]{2,1,0:T(8,128)(2,1)S(1)}, bf16[2,256,128]{2,1,0:T(8,128)(2,1)}, u32[]{:S(2)}) copy-start(bf16[2,256,128]{2,1,0:T(8,128)(2,1)} %param.15) | copy-start | bytes 393220
  350.8 6.2 %copy-start.7 = (bf16[1024,128]{1,0:T(8,128)(2,1)S(1)}, bf16[1024,128]{1,0:T(8,128)(2,1)}, u32[]{:S(2)}) copy-start(bf16[1024,128]{1,0:T(8,128)(2,1)} %param.23) | copy-start | bytes 786436
Sparse Core Ops, SparseCore 0:
  62.7 36.0 all-gather.3
  263.1 78.1 all-gather.5
where the time goes:
time: 368 us; the launch traced here: 365 us
  waiting for transfers between devices  124 us (34%)
  local copies, waits for them, and re-layouts  60.6 us (16%)
  matrix products  52.1 us (14%)
  blocking collectives  51.8 us (14%)
  Pallas kernels  30.7 us (8%)
  other arithmetic  16.8 us (5%)
  starting transfers between devices  14.8 us (4%)
  between operations  14.4 us (4%)
    all_gather x1, waiting for transfers between devices, shards(): piece = lax.all_gather(right, DAP, axis=1, tiled=True)  77.3 us
    all_gather x2, blocking collectives, stacked_from(): tiles = lax.all_gather(tiles, axes[k], axis=0, tiled=True)  51.8 us
    dot_general x8, Pallas kernels, one_head(): jnp.einsum('bij,bjd->bid', weights, vh, preferred_element_type=jnp.float32)  30.7 us
    all_gather x1, waiting for transfers between devices, stacked_from(): tiles = lax.all_gather(tiles, axes[k], axis=0, tiled=True)  27.3 us
    dynamic_slice x40, local copies, waits for them, and re-layouts, attend(): lax.map(one_head, (jnp.moveaxis(query, 2, 0), jnp.moveaxis(keys, 2, 0), j...  27.3 us
    all_to_all x1, waiting for transfers between devices, shards(): lax.all_to_all(homolog_later, DAP, split_axis=1, concat_axis=0, tiled=True)  18.9 us
    dynamic_update_slice x16, local copies, waits for them, and re-layouts, attend(): lax.map(one_head, (jnp.moveaxis(query, 2, 0), jnp.moveaxis(keys, 2, 0), j...  15 us
    dot_general x8, matrix products, one_head(): jnp.einsum('bij,bjd->bid', weights, vh, preferred_element_type=jnp.float32)  14.8 us
  transfers between devices with their start and end apart: 3, of which 3 were waited for; matrix products, arithmetic and copies ran while one was open for 2% of the time, Pallas kernels for 0%

commit v1 on v0

--- a/solution.py
+++ b/solution.py
@@ -113,7 +113,9 @@
     right = factors[..., FACTOR_FEATURES:].astype(jnp.bfloat16)
     total = left.shape[0]
     own_rows = left.shape[1]
-    piece = lax.all_gather(right, DAP, axis=1, tiled=True)
+    piece = jnp.concatenate(
+        lax.all_to_all(jnp.stack([right] * lax.axis_size(DAP)), DAP, 0, 0), axis=1
+    )
     outer = jnp.einsum("sic,sjd->ijcd", left, piece, preferred_element_type=jnp.float32) / total
     outer = outer.astype(jnp.bfloat16).reshape(
         own_rows, piece.shape[1], FACTOR_FEATURES * FACTOR_FEATURES

time: 368 us -> 531 us (1.44)
  the two profiles are of different devices: /device:TPU:513 before, /device:TPU:523 now
where the time goes in v1:
time: 531 us; the launch traced here: 529 us
  waiting for transfers between devices  272 us (51%)
  local copies, waits for them, and re-layouts  64.3 us (12%)
  matrix products  52.1 us (10%)
  blocking collectives  47.1 us (9%)
  Pallas kernels  30.7 us (6%)
  starting transfers between devices  30.5 us (6%)
  other arithmetic  16.8 us (3%)
  between operations  14.4 us (3%)
    all_to_all x1, waiting for transfers between devices, shards(): lax.all_to_all(jnp.stack([right] * lax.axis_size(DAP)), DAP, 0, 0)  228 us
    all_gather x2, blocking collectives, stacked_from(): tiles = lax.all_gather(tiles, axes[k], axis=0, tiled=True)  47.1 us
    dot_general x8, Pallas kernels, one_head(): jnp.einsum('bij,bjd->bid', weights, vh, preferred_element_type=jnp.float32)  30.7 us
    all_gather x1, waiting for transfers between devices, stacked_from(): tiles = lax.all_gather(tiles, axes[k], axis=0, tiled=True)  29.6 us
    dynamic_slice x40, local copies, waits for them, and re-layouts, attend(): lax.map(one_head, (jnp.moveaxis(query, 2, 0), jnp.moveaxis(keys, 2, 0), j...  27.3 us
    all_to_all x1, starting transfers between devices, shards(): lax.all_to_all(homolog_later, DAP, split_axis=1, concat_axis=0, tiled=True)  16.8 us
    dynamic_update_slice x16, local copies, waits for them, and re-layouts, attend(): lax.map(one_head, (jnp.moveaxis(query, 2, 0), jnp.moveaxis(keys, 2, 0), j...  15 us
    dot_general x8, matrix products, one_head(): jnp.einsum('bij,bjd->bid', weights, vh, preferred_element_type=jnp.float32)  14.8 us
  transfers between devices with their start and end apart: 3, of which 3 were waited for; matrix products, arithmetic and copies ran while one was open for 2% of the time, Pallas kernels for 0%

profile of v1, /device:TPU:523, one launch (start us, length us, event | category | flops | bytes accessed | tf_op | source)
XLA Modules:
  0.0 528.6 jit_solution(4830372524008518074)
XLA Ops:
  10.7 17.0 %all-gather = bf16[64,2,256]{2,0,1:T(8,128)(2,1)S(1)} all-gather(bf16[8,2,256]{2,0,1:T(8,128)(2,1)S(1)} %fusion.33), channel_id=2, replica_groups=mesh['groups'=2,'dap_0'=8,'dap_1'=8,'dap_2'=2] {'dap_0'}, dimensions={0}, use_global_device_ids=true | all-gather | bytes 73728 | tf_op jit(solution)/shard_map/all_gather | solution.py:23
  27.8 30.1 %all_gather.10 = bf16[64,8,2,256]{3,1,0,2:T(8,128)(2,1)} all-gather(bf16[8,8,2,256]{3,1,0,2:T(8,128)(2,1)S(1)} %bitcast.195), channel_id=1, replica_groups=mesh['groups'=2,'dap_0'=8,'dap_1'=8,'dap_2'=2] {'dap_1'}, dimensions={0}, use_global_device_ids=true | all-gather | bytes 589824 | tf_op jit(solution)/shard_map/all_gather | solution.py:23
  60.7 2.0 fusion.55
  66.8 29.6 %all-gather.3.cloned.1.call-done = bf16[128,8,2,256]{3,1,0,2:T(8,128)(2,1)} async-done(((bf16[64,8,2,256]{3,1,0,2:T(8,128)(2,1)}), bf16[128,8,2,256]{3,1,0,2:T(8,128)(2,1)}) %all-gather.3.cloned.1.call-update) | async-done | bytes 1048592 | tf_op jit(solution)/shard_map/all_gather | solution.py:23
  98.5 35.9 %while.20 = (s32[]{:T(128)}, f32[8,4,256,32]{2,3,0,1:T(8,128)}, bf16[8,4,256,32]{2,3,0,1:T(8,128)(2,1)}, bf16[8,4,256,32]{2,3,0,1:T(8,128)(2,1)}, bf16[8,256,256...) while((s32[]{:T(128)}, f32[8,4,256,32]{2,3,0,1:T(8,128)}, ...), condition=%wide.region_7.8_spmd, body=%wide.region_4.7_spmd.sunk | while | flops 52233728 | bytes 4533337 | solution.py:59
  101.2 1.9 fusion.102
  105.7 1.9 fusion.102
  110.2 1.9 fusion.102
  114.7 1.8 fusion.102
  119.2 1.8 fusion.102
  123.7 1.8 fusion.102
  128.1 1.8 fusion.102
  132.6 1.9 fusion.102
  134.5 1.8 fusion.50
  138.8 16.8 %all-to-all-start = ((bf16[4,256,256]{2,0,1:T(4,128)(2,1)}), bf16[4,256,256]{2,0,1:T(4,128)(2,1)S(1)}, u32[]{:S(2)}, u32[]{:S(2)}) async-start(bf16[4,256,256]{2,0,1:T(4,128)(2,1)} %copy.59), calls=%async_computation | async-start | bytes 1048576 | tf_op jit(solution)/shard_map/all_to_all | solution.py:97
  155.6 14.8 %all-to-all-done = bf16[4,256,256]{2,0,1:T(4,128)(2,1)S(1)} async-done(((bf16[4,256,256]{2,0,1:T(4,128)(2,1)}), bf16[4,256,256]{2,0,1:T(4,128)(2,1)S(1)}, u32[]{:S(2)}, u32[]{:S(2)}) %all-to-all-start) | async-done | bytes 524320 | tf_op jit(solution)/shard_map/all_to_all | solution.py:97
  180.0 2.1 slice_bitcast_fusion
  182.1 73.0 %while.21 = (s32[]{:T(128)}, f32[8,2,512,32]{2,3,0,1:T(8,128)}, bf16[8,2,512,32]{2,3,0,1:T(8,128)(2,1)S(1)}, bf16[8,2,512,32]{2,3,0,1:T(8,128)(2,1)}, bf16[8,2,512,32]{2,3,0,1:T(8,128)(2,1)S(1)}, /*index=5*/s32[]{:T(128)}) while((s32[]{:T(128)}, f32[8,2,512,32]{2,3,0,1:T(8,128)}, bf16[8,2,512,32]{2,3,0,1:T(8,128)(2,1)S(1)}, ...), condition=%wide.region_13.14_spmd, body=%wide.region_10.13_spmd.sunk | while | flops 67108864 | bytes 1507417 | solution.py:59
  185.5 3.8 dot_general.47
  194.6 3.8 dot_general.47
  203.8 3.8 dot_general.47
  212.9 3.8 dot_general.47
  222.0 3.8 dot_general.47
  231.1 3.8 dot_general.47
  240.3 3.8 dot_general.47
  249.4 3.8 dot_general.47
  255.1 1.8 fusion.51
  257.8 4.3 stack.2
  262.1 13.7 %all-to-all-start.1 = ((bf16[128,512,2,32]{1,3,2,0:T(8,128)(2,1)}), bf16[128,512,2,32]{1,3,2,0:T(8,128)(2,1)}, u32[]{:S(2)}, u32[]{:S(2)}) async-start(bf16[128,512,2,32]{1,3,2,0:T(8,128)(2,1)} %stack.2), calls=%async_computation.1 | async-start | bytes 16777216 | tf_op jit(solution)/shard_map/all_to_all | solution.py:117
  276.8 228.1 %all-to-all-done.1 = bf16[128,512,2,32]{1,3,2,0:T(8,128)(2,1)} async-done(((bf16[128,512,2,32]{1,3,2,0:T(8,128)(2,1)}), bf16[128,512,2,32]{1,3,2,0:T(8,128)(2,1)}, u32[]{:S(2)}, u32[]{:S(2)}) %all-to-all-start.1) | async-done | bytes 8388640 | tf_op jit(solution)/shard_map/all_to_all | solution.py:117
  504.9 9.4 %fusion.24 = bf16[2,256,32,32]{2,3,0,1:T(8,128)(2,1)} fusion(bf16[512,256,32,1]{0,2,3,1:T(8,128)(2,1)} %bitcast.52, bf16[512,2,64]{0,2,1:T(8,128)(2,1)S(1)} %convolution_convert_fusion), kind=kOutput, calls=%fused_computation.28 | convolution fusion | flops 537919488 | bytes 9502720 | tf_op jit(solution)/shard_map/sic,sjd->ijcd/dot_general | solution.py:119
  514.4 6.2 %copy.71 = bf16[2,256,32,32]{1,3,2,0:T(8,128)(2,1)S(1)} copy(bf16[2,256,32,32]{2,3,0,1:T(8,128)(2,1)} %fusion.24) | data formatting | bytes 2097152 | tf_op jit(solution)/shard_map/convert_element_type | solution.py:120
  (141 shorter events, 90.9 us)
Async XLA Ops:
  7.2 53.5 %copy-start = (bf16[256,1024]{1,0:T(8,128)(2,1)S(1)}, bf16[256,1024]{1,0:T(8,128)(2,1)}, u32[]{:S(2)}) copy-start(bf16[256,1024]{1,0:T(8,128)(2,1)} %param.18) | copy-start | bytes 1572868
  7.2 89.2 %all-gather.3.cloned.1.call-start = ((), (), s32[]{:S(2)}) async-start(), calls=%async_computation.2 | async-start | bytes 1572864 | tf_op jit(solution)/shard_map/all_gather | solution.py:23
  62.7 3.0 copy-start.2
  62.7 1.1 copy-start.6
  98.5 37.8 %copy-start.3 = (bf16[4,256,256]{2,1,0:T(8,128)(2,1)S(1)}, bf16[4,256,256]{2,1,0:T(8,128)(2,1)}, u32[]{:S(2)}) copy-start(bf16[4,256,256]{2,1,0:T(8,128)(2,1)} %param.14) | copy-start | bytes 1572868
  98.5 37.8 %copy-start.9 = (bf16[256,256]{1,0:T(8,128)(2,1)S(1)}, bf16[256,256]{1,0:T(8,128)(2,1)}, u32[]{:S(2)}) copy-start(bf16[256,256]{1,0:T(8,128)(2,1)} %param.19) | copy-start | bytes 393220
  138.8 36.0 %copy-start.5 = (bf16[256,1024]{1,0:T(8,128)(2,1)S(1)}, bf16[256,1024]{1,0:T(8,128)(2,1)}, u32[]{:S(2)}) copy-start(bf16[256,1024]{1,0:T(8,128)(2,1)} %param.20) | copy-start | bytes 1572868
  138.8 31.5 %all-to-all-start = ((bf16[4,256,256]{2,0,1:T(4,128)(2,1)}), bf16[4,256,256]{2,0,1:T(4,128)(2,1)S(1)}, u32[]{:S(2)}, u32[]{:S(2)}) async-start(bf16[4,256,256]{2,0,1:T(4,128)(2,1)} %copy.59), calls=%async_computation | async-start | bytes 1048576 | tf_op jit(solution)/shard_map/all_to_all | solution.py:97
  175.6 1.9 copy-start.1
  182.1 74.9 %copy-start.8 = (bf16[256,256]{1,0:T(8,128)(2,1)S(1)}, bf16[256,256]{1,0:T(8,128)(2,1)}, u32[]{:S(2)}) copy-start(bf16[256,256]{1,0:T(8,128)(2,1)} %param.21) | copy-start | bytes 393220
  255.1 2.4 copy-start.10
  262.1 242.9 %all-to-all-start.1 = ((bf16[128,512,2,32]{1,3,2,0:T(8,128)(2,1)}), bf16[128,512,2,32]{1,3,2,0:T(8,128)(2,1)}, u32[]{:S(2)}, u32[]{:S(2)}) async-start(bf16[128,512,2,32]{1,3,2,0:T(8,128)(2,1)} %stack.2), calls=%async_computation.1 | async-start | bytes 16777216 | tf_op jit(solution)/shard_map/all_to_all | solution.py:117
  514.4 6.2 %copy-start.4 = (bf16[2,256,128]{2,1,0:T(8,128)(2,1)S(1)}, bf16[2,256,128]{2,1,0:T(8,128)(2,1)}, u32[]{:S(2)}) copy-start(bf16[2,256,128]{2,1,0:T(8,128)(2,1)} %param.15) | copy-start | bytes 393220
  514.4 6.2 %copy-start.7 = (bf16[1024,128]{1,0:T(8,128)(2,1)S(1)}, bf16[1024,128]{1,0:T(8,128)(2,1)}, u32[]{:S(2)}) copy-start(bf16[1024,128]{1,0:T(8,128)(2,1)} %param.23) | copy-start | bytes 786436
Sparse Core Ops, SparseCore 0:
  58.0 38.2 all-gather.2
